TPU v7x, 128 devices: a whole 4x4x4 slice. The times are simulated.
128 devices in a mesh: dp: 16 (over x, y), mp: 8 (over z, core).
Axes of the slice: x: 4, y: 4, z: 4, core: 2. Of those that a mesh axis runs over, the one named last changes fastest.
Arguments:
- patches: bfloat16 [768, 64, 1024], P(('dp', 'mp')), may hold values from -6 to 6
- gain_first: float32 [1024], replicated, may hold values from 0.1 to 1.9
- joint_weight: bfloat16 [1024, 3, 1024], P('dp', None, 'mp'), may hold values from -0.1875 to 0.1875
- head_scale: float32 [16], P('mp'), may hold values from 2 to 32
- output_weight: bfloat16 [1024, 1024], P('mp', 'dp'), may hold values from -0.1875 to 0.1875
- gain_second: float32 [1024], replicated, may hold values from 0.3 to 3
- up_weight: bfloat16 [1024, 4096], P('dp', 'mp'), may hold values from -0.1875 to 0.1875
- down_weight: bfloat16 [4096, 1024], P('mp', 'dp'), may hold values from -0.09375 to 0.09375
- gain_final: float32 [1024], replicated, may hold values from 0.1 to 1.9
- project_weight: bfloat16 [1024, 768], replicated, may hold values from -0.1875 to 0.1875
- text_bank: bfloat16 [12288, 768], P(('dp', 'mp')), may hold values from -20000 to 20000
- captions: int32 [768], replicated, may hold values from 0 to 12287
- reference_loss: float32 [768], P(('dp', 'mp')), may hold values from 2 to 20
Outputs:
- learnability: float32 [768], P(('dp', 'mp'))
All inputs are finite; a program needn't handle non-finite values.
Results may differ from a plain program's by a relative error of at most 0.018.
Values may be sent and summed in bfloat16 or wider, within the bound.
No kernel may reach another device: no remote copies, remote signals or barrier semaphores. Data moves between devices by JAX's collectives and lax.ppermute only.
A program may use at most 128 MiB of HBM per device.

v0:
```python
import jax
import jax.numpy as jnp
from jax import lax
from jax.sharding import PartitionSpec as P


def gather_turned(arrays, axis, dims):
    turned = [jnp.moveaxis(a, dim, 0) for a, dim in zip(arrays, dims)]
    both = jnp.concatenate([t.reshape(len(t), -1) for t in turned], axis=1)
    result, at, outs = (lax.all_gather(both, axis, axis=0, tiled=True), 0, [])
    for t, dim in zip(turned, dims):
        slab = result[:, at : at + t[0].size].reshape(-1, *t.shape[1:])
        outs.append(jnp.moveaxis(slab, 0, dim))
        at += t[0].size
    return tuple(outs)


def joined_along(parts, dim):
    lengths = list(parts.shape[1:])
    lengths[dim] *= parts.shape[0]
    return jnp.moveaxis(parts, 0, dim).reshape(lengths)


def sent_to_all(array, axis):
    devices = lax.axis_size(axis)
    return lax.all_to_all(
        jnp.broadcast_to(array[None], (devices, *array.shape)), axis, 0, 0, tiled=True
    )


def gathered_copies(array, axis, dim):
    return joined_along(sent_to_all(array, axis), dim)


def layer_norm(values, gain):
    centre = values - jnp.mean(values, axis=-1, keepdims=True)
    spread = jnp.mean(centre * centre, axis=-1, keepdims=True)
    return centre * lax.rsqrt(spread + 1e-06) * gain


def unit_rows(values):
    return values * lax.rsqrt(jnp.sum(values * values, axis=-1, keepdims=True) + 1e-06)


def attend(normed_rows, joint_full, scales, image_count, patch_count):
    features = normed_rows.shape[1]
    local_heads = scales.shape[0]
    head_width = joint_full.shape[2] // local_heads
    joint = jnp.dot(
        normed_rows, joint_full.reshape(features, -1), preferred_element_type=jnp.float32
    )
    joint = joint.reshape(image_count, patch_count, 3, local_heads, head_width)
    queries = unit_rows(joint[:, :, 0]).astype(jnp.bfloat16)
    key_rows = unit_rows(joint[:, :, 1]).astype(jnp.bfloat16)
    value_rows = joint[:, :, 2].astype(jnp.bfloat16)
    scores = jnp.einsum("bqhd,bkhd->bhqk", queries, key_rows, preferred_element_type=jnp.float32)
    exponent = jnp.exp(scores * scales[None, :, None, None])
    attention = (exponent / jnp.sum(exponent, axis=-1, keepdims=True)).astype(jnp.bfloat16)
    head_out = jnp.einsum(
        "bhqk,bkhd->bqhd", attention, value_rows, preferred_element_type=jnp.float32
    ).astype(jnp.bfloat16)
    return head_out.reshape(image_count * patch_count, local_heads * head_width)


def grouped_local(left_rows, right_cols, groups):
    rows = left_rows.shape[0]
    group_width = left_rows.shape[1] // groups
    left_groups = left_rows.reshape(rows, groups, group_width)
    right_groups = right_cols.reshape(groups, group_width, right_cols.shape[1])
    partial_value = jnp.einsum(
        "rgk,gkn->rgn", left_groups, right_groups, preferred_element_type=jnp.float32
    )
    rounded = lax.optimization_barrier(partial_value.astype(jnp.bfloat16))
    return jnp.sum(rounded.astype(jnp.float32), axis=1)


def shards(
    patches,
    gain_first,
    joint_weight,
    head_scale,
    output_weight,
    gain_second,
    up_weight,
    down_weight,
    gain_final,
    project_weight,
    text_bank,
    captions,
    reference_loss,
):
    joint_full, output_full, up_full, down_full = gather_turned(
        (joint_weight, output_weight, up_weight, down_weight), "dp", (0, 1, 0, 1)
    )
    own_images, patch_count, features = patches.shape
    residual = patches.astype(jnp.float32)
    normed_first = layer_norm(residual, gain_first).astype(jnp.bfloat16)
    groups = lax.axis_size("mp")
    joint_all, output_all, up_all, down_all = (
        lax.all_gather(joint_full, "mp", axis=2, tiled=True),
        lax.all_gather(output_full, "mp", axis=0, tiled=True),
        lax.all_gather(up_full, "mp", axis=1, tiled=True),
        lax.all_gather(down_full, "mp", axis=0, tiled=True),
    )
    scales_all = gathered_copies(head_scale, "mp", 0)
    flat_rows = normed_first.reshape(own_images * patch_count, features)
    head_out = attend(flat_rows, joint_all, scales_all, own_images, patch_count)
    residual_flat = residual.reshape(own_images * patch_count, features)
    residual_two = residual_flat + grouped_local(head_out, output_all, groups)
    normed_second = layer_norm(residual_two, gain_second).astype(jnp.bfloat16)
    upper = jnp.dot(normed_second, up_all, preferred_element_type=jnp.float32)
    hidden = jax.nn.gelu(upper, approximate=False).astype(jnp.bfloat16)
    feed = grouped_local(hidden, down_all, groups)
    pooled = (
        jnp.sum((residual_two + feed).reshape(own_images, patch_count, features), axis=1)
        / patch_count
    )
    pooled_norm = layer_norm(pooled, gain_final).astype(jnp.bfloat16)
    embedded = jnp.dot(pooled_norm, project_weight, preferred_element_type=jnp.float32)
    image_units = unit_rows(embedded).astype(jnp.bfloat16)
    first_row = lax.axis_index(("dp", "mp")) * own_images
    own_captions = lax.dynamic_slice_in_dim(captions, first_row, own_images)
    highest = jnp.full((own_images,), -1e30, jnp.float32)
    logits = lax.dot_general(
        image_units,
        lax.all_gather(text_bank, ("dp", "mp"), axis=0, tiled=True),
        (((1,), (1,)), ((), ())),
        preferred_element_type=jnp.float32,
    )
    new_highest = jnp.maximum(highest, jnp.max(logits, axis=1))
    totals = jnp.sum(jnp.exp(logits - new_highest[:, None]), axis=1)
    text_ids = lax.broadcasted_iota(jnp.int32, logits.shape, 1)
    matched = jnp.sum(jnp.where(text_ids == own_captions[:, None], logits, 0.0), axis=1)
    highest, totals, matched = (new_highest, totals, matched)
    return highest + jnp.log(totals) - matched - reference_loss


def solution(mesh):
    placed = (
        P(("dp", "mp"), None, None),
        P(),
        P("dp", None, "mp"),
        P("mp"),
        P("mp", "dp"),
        P(),
        P("dp", "mp"),
        P("mp", "dp"),
        P(),
        P(),
        P(("dp", "mp"), None),
        P(),
        P(("dp", "mp")),
    )
    return jax.shard_map(
        shards, mesh=mesh, in_specs=placed, out_specs=P(("dp", "mp")), check_vma=False
    )
```

profile of v0, /device:TPU:1, one launch (start us, length us, event | category | flops | bytes accessed | tf_op | source)
XLA Modules:
  0.0 336.5 jit_solution(14013959427415211761)
XLA Ops:
  7.5 1.6 pad_maximum_fusion
  9.1 50.7 %all-gather.7.cloned.1.call-done = bf16[1024,1536]{1,0:T(8,128)(2,1)} async-done(((bf16[64,1536]{1,0:T(8,128)(2,1)}), bf16[1024,1536]{1,0:T(8,128)(2,1)}) %all-gather.7.cloned.1.call-update) | async-done | bytes 3145744 | tf_op jit(solution)/shard_map/all_gather | solution.py:10
  59.8 1.2 slice.30
  61.0 1.2 copy.85
  62.3 1.0 slice.29
  64.2 2.7 fusion.42
  66.9 1.3 copy.86
  69.5 5.7 %all-to-all-start = ((f32[8,1,2]{2,1,0:T(1,128)}), f32[8,1,2]{2,1,0:T(1,128)S(1)}, u32[]{:S(2)}, u32[]{:S(2)}) async-start(f32[8,1,2]{2,1,0:T(1,128)} %broadcast_in_dim.5), calls=%async_computation | async-start | bytes 8192 | tf_op jit(solution)/shard_map/all_to_all | solution.py:26
  75.2 1.4 copy.74
  77.9 2.1 all-to-all-done
  81.3 22.1 %all-gather.11.cloned.1.call-done = bf16[1024,3,1024]{0,2,1:T(8,128)(2,1)} async-done(((bf16[1024,3,128]{0,2,1:T(8,128)(2,1)}), bf16[1024,3,1024]{0,2,1:T(8,128)(2,1)}) %all-gather.11.cloned.1.call-update) | async-done | bytes 6291472 | tf_op jit(solution)/shard_map/all_gather | solution.py:100
  103.3 8.1 %fusion.23 = f32[6,64,3,16,64]{1,4,3,2,0:T(8,128)S(1)} fusion(bf16[3,16,64,1024,1]{3,2,1,0,4:T(8,128)(2,1)} %bitcast.81, bf16[6,64,1024]{2,1,0:T(8,128)(2,1)S(1)} %copy-done.1, f32[1024]{0:T(1024)S(1)} %copy-done.5, f32[6,64]{1,0:T(8,128)S(1)} %add_rsqrt_fusion.3, f32[6,64]{1,0:T(8,128)S(1)} %broadcast_multiply_fusion.1), kind=kOutput, calls=%fused_computation.50 | convolution fusion | flops 2417885184 | bytes 11803648 | tf_op jit(solution)/shard_map/dot_general | solution.py:49
  111.4 1.2 multiply_reduce_fusion.1
  112.7 1.2 fusion.12
  113.9 2.0 fusion.19
  115.9 3.2 copy.69
  119.0 2.6 reshape_reshape.3
  121.7 8.8 %all-gather.9.cloned.1.call-done = bf16[1024,1024]{1,0:T(8,128)(2,1)} async-done(((bf16[128,1024]{1,0:T(8,128)(2,1)}), bf16[1024,1024]{1,0:T(8,128)(2,1)}) %all-gather.9.cloned.1.call-update) | async-done | bytes 2097168 | tf_op jit(solution)/shard_map/all_gather | solution.py:101
  130.5 3.5 %convert_bitcast_fusion.1 = bf16[384,8,1024]{0,2,1:T(8,128)(2,1)S(1)} fusion(bf16[8,128,1024]{2,1,0:T(8,128)(2,1)} %bitcast.76, bf16[384,8,128]{2,1,0:T(8,128)(2,1)S(1)} %reshape_reshape.3), kind=kOutput, calls=%fused_computation.20 | convolution fusion | flops 808452096 | bytes 9175040 | tf_op jit(solution)/shard_map/rgk,gkn->rgn/dot_general | solution.py:70
  134.0 2.0 convert_reduce_fusion.1
  136.0 3.0 copy.72
  139.0 1.6 fusion.33
  140.7 1.9 multiply_reduce_fusion.2
  142.7 39.5 %all-gather.15.cloned.1.call-done = bf16[1024,4096]{1,0:T(8,128)(2,1)} async-done(((bf16[1024,512]{1,0:T(8,128)(2,1)}), bf16[1024,4096]{1,0:T(8,128)(2,1)}) %all-gather.15.cloned.1.call-update) | async-done | bytes 8388624 | tf_op jit(solution)/shard_map/all_gather | solution.py:102
  182.2 21.2 %fusion.2 = bf16[384,4096]{1,0:T(8,128)(2,1)} fusion(bf16[1024,4096]{1,0:T(8,128)(2,1)} %all-gather.15.cloned.1.call-done, f32[384,1024]{0,1:T(8,128)} %copy.74, f32[384,1024]{0,1:T(8,128)} %convert_reduce_fusion.1, f32[1024]{0:T(1024)S(1)} %copy-done.6, f32[384]{0:T(512)S(1)} %rsqrt.55, f32[384]{0:T(512)S(1)} %div.39), kind=kOutput, calls=%fused_computation.5 | convolution fusion | flops 3325427712 | bytes 14687232 | tf_op jit(solution)/shard_map/dot_general | solution.py:111
  203.4 30.3 %all-gather.13.cloned.1.call-done = bf16[4096,1024]{1,0:T(8,128)(2,1)} async-done(((bf16[512,1024]{1,0:T(8,128)(2,1)}), bf16[4096,1024]{1,0:T(8,128)(2,1)}) %all-gather.13.cloned.1.call-update) | async-done | bytes 8388624 | tf_op jit(solution)/shard_map/all_gather | solution.py:103
  233.7 11.9 %convert_bitcast_fusion = bf16[384,8,1024]{0,2,1:T(8,128)(2,1)} fusion(bf16[8,512,1024]{2,1,0:T(8,128)(2,1)} %bitcast.80, bf16[48,8,8,512]{3,2,1,0:T(8,128)(2,1)} %bitcast.82), kind=kOutput, calls=%fused_computation.6 | convolution fusion | flops 3224371200 | bytes 17825792 | tf_op jit(solution)/shard_map/rgk,gkn->rgn/dot_general | solution.py:70
  245.6 5.1 %convert_reduce_fusion = f32[384,1024]{0,1:T(8,128)} fusion(bf16[384,8,1024]{0,2,1:T(8,128)(2,1)} %convert_bitcast_fusion), kind=kLoop, calls=%fused_computation | loop fusion | flops 5898240 | bytes 7864320 | tf_op jit(solution)/shard_map/reduce_sum | solution.py:74
  250.6 3.0 copy.77
  253.7 2.3 add_reduce_fusion
  256.8 62.9 %all-gather.17.cloned.1.call-done = bf16[12288,768]{1,0:T(8,128)(2,1)} async-done(((bf16[96,768]{1,0:T(8,128)(2,1)}), bf16[12288,768]{1,0:T(8,128)(2,1)}) %all-gather.17.cloned.1.call-update) | async-done | bytes 18874384 | tf_op jit(solution)/shard_map/all_gather | solution.py:126
  319.7 9.0 %fusion.43 = (f32[6]{0:T(128)S(1)}, f32[6,12288]{1,0:T(8,128)S(1)}) fusion(bf16[12288,768]{1,0:T(8,128)(2,1)} %all-gather.17.cloned.1.call-done, f32[6,768]{1,0:T(8,128)S(1)} %get-tuple-element.14, f32[6]{0:T(128)S(1)} %add_rsqrt_fusion.4), kind=kOutput, calls=%fused_computation.90 | convolution fusion | flops 113329144 | bytes 19187760 | tf_op jit(solution)/shard_map/dot_general | solution.py:124
  (51 shorter events, 7.6 us)
Async XLA Ops:
  6.5 249.8 %copy-start = (bf16[1024,768]{1,0:T(8,128)(2,1)S(1)}, bf16[1024,768]{1,0:T(8,128)(2,1)}, u32[]{:S(2)}) copy-start(bf16[1024,768]{1,0:T(8,128)(2,1)} %param.22) | copy-start | bytes 4718596
  6.5 53.2 %all-gather.7.cloned.1.call-start = ((), (), s32[]{:S(2)}) async-start(), calls=%async_computation.1 | async-start | bytes 3342336 | tf_op jit(solution)/shard_map/all_gather | solution.py:10
  9.1 94.3 %all-gather.11.cloned.1.call-start = ((), (), s32[]{:S(2)}) async-start(), calls=%async_computation.3 | async-start | bytes 7077888 | tf_op jit(solution)/shard_map/all_gather | solution.py:100
  61.0 7.9 %copy-start.3 = (f32[2]{0:T(128)S(1)}, f32[2]{0:T(128)}, u32[]{:S(2)}) copy-start(f32[2]{0:T(128)} %param.16) | copy-start | bytes 28
  61.0 14.2 %copy-start.1 = (bf16[6,64,1024]{2,1,0:T(8,128)(2,1)S(1)}, bf16[6,64,1024]{2,1,0:T(8,128)(2,1)}, u32[]{:S(2)}) copy-start(bf16[6,64,1024]{2,1,0:T(8,128)(2,1)} %param.13) | copy-start | bytes 2359300
  62.2 68.3 %all-gather.9.cloned.1.call-start = ((), (), s32[]{:S(2)}) async-start(), calls=%async_computation.2 | async-start | bytes 2359296 | tf_op jit(solution)/shard_map/all_gather | solution.py:101
  64.1 39.2 %copy-start.5 = (f32[1024]{0:T(1024)S(1)}, f32[1024]{0:T(1024)}, u32[]{:S(2)}) copy-start(f32[1024]{0:T(1024)} %param.14) | copy-start | bytes 12292
  64.1 118.1 %all-gather.15.cloned.1.call-start = ((), (), s32[]{:S(2)}) async-start(), calls=%async_computation.5 | async-start | bytes 9437184 | tf_op jit(solution)/shard_map/all_gather | solution.py:102
  66.9 166.8 %all-gather.13.cloned.1.call-start = ((), (), s32[]{:S(2)}) async-start(), calls=%async_computation.4 | async-start | bytes 9437184 | tf_op jit(solution)/shard_map/all_gather | solution.py:103
  68.3 251.4 %all-gather.17.cloned.1.call-start = ((), (), s32[]{:S(2)}) async-start(), calls=%async_computation.6 | async-start | bytes 19021824 | tf_op jit(solution)/shard_map/all_gather | solution.py:126
  69.5 10.5 %all-to-all-start = ((f32[8,1,2]{2,1,0:T(1,128)}), f32[8,1,2]{2,1,0:T(1,128)S(1)}, u32[]{:S(2)}, u32[]{:S(2)}) async-start(f32[8,1,2]{2,1,0:T(1,128)} %broadcast_in_dim.5), calls=%async_computation | async-start | bytes 8192 | tf_op jit(solution)/shard_map/all_to_all | solution.py:26
  134.0 48.2 %copy-start.6 = (f32[1024]{0:T(1024)S(1)}, f32[1024]{0:T(1024)}, u32[]{:S(2)}) copy-start(f32[1024]{0:T(1024)} %param.18) | copy-start | bytes 12292
  245.6 10.8 %copy-start.2 = (f32[1024]{0:T(1024)S(1)}, f32[1024]{0:T(1024)}, u32[]{:S(2)}) copy-start(f32[1024]{0:T(1024)} %param.21) | copy-start | bytes 12292
  319.7 9.4 %copy-start.4 = (f32[6]{0:T(128)S(1)}, f32[6]{0:T(128)}, u32[]{:S(2)}) copy-start(f32[6]{0:T(128)} %param.25) | copy-start | bytes 76
Sparse Core Ops, SparseCore 0:
  9.5 50.2 all-gather.6
  62.3 40.9 all-gather.10
  105.0 25.4 all-gather.8
  132.0 50.1 all-gather.14
  183.8 49.8 all-gather.12
  236.6 83.0 all-gather.16
where the time goes:
time: 337 us; the launch traced here: 336 us
  waiting for transfers between devices  217 us (64%)
  matrix products  57.3 us (17%)
  local copies, waits for them, and re-layouts  24.5 us (7%)
  other arithmetic  18.1 us (5%)
  between operations  13.7 us (4%)
  starting transfers between devices  5.93 us (2%)
    all_gather x1, waiting for transfers between devices, shards(): lax.all_gather(text_bank, ('dp', 'mp'), axis=0, tiled=True)  62.9 us
    all_gather x1, waiting for transfers between devices, gather_turned(): result, at, outs = (lax.all_gather(both, axis, axis=0, tiled=True), 0, [])  50.7 us
    all_gather x1, waiting for transfers between devices, shards(): lax.all_gather(up_full, 'mp', axis=1, tiled=True)  39.5 us
    all_gather x1, waiting for transfers between devices, shards(): lax.all_gather(down_full, 'mp', axis=0, tiled=True)  30.3 us
    all_gather x1, waiting for transfers between devices, shards(): lax.all_gather(joint_full, 'mp', axis=2, tiled=True)  22.1 us
    dot_general x1, matrix products, shards(): upper = jnp.dot(normed_second, up_all, preferred_element_type=jnp.float32)  21.2 us
    dot_general x2, matrix products, grouped_local(): jnp.einsum('rgk,gkn->rgn', left_groups, right_groups, preferred_element_t...  15.4 us
    dot_general x1, matrix products, shards(): lax.dot_general(image_units, lax.all_gather(text_bank, ('dp', 'mp'), axis...  9.03 us
  transfers between devices with their start and end apart: 7, of which 7 were waited for; matrix products, arithmetic and copies ran while one was open for 25% of the time, Pallas kernels for 0%

commit v1 on v0

--- a/solution.py
+++ b/solution.py
@@ -2,6 +2,11 @@
 import jax.numpy as jnp
 from jax import lax
 from jax.sharding import PartitionSpec as P
+from jax.lax import all_gather
+
+
+def shape_sources_all(mine_x, peer_axis):
+    return jnp.concatenate(all_gather(mine_x, peer_axis), axis=2)
 
 
 def gather_turned(arrays, axis, dims):
@@ -97,7 +102,7 @@
     normed_first = layer_norm(residual, gain_first).astype(jnp.bfloat16)
     groups = lax.axis_size("mp")
     joint_all, output_all, up_all, down_all = (
-        lax.all_gather(joint_full, "mp", axis=2, tiled=True),
+        shape_sources_all(joint_full, "mp"),
         lax.all_gather(output_full, "mp", axis=0, tiled=True),
         lax.all_gather(up_full, "mp", axis=1, tiled=True),
         lax.all_gather(down_full, "mp", axis=0, tiled=True),

time: 337 us -> 338 us (level)
  waiting for transfers between devices: 217 us -> 208 us
  local copies, waits for them, and re-layouts: 24.5 us -> 33.4 us
    all_gather x1, waiting for transfers between devices: 8.83 us -> 0.17 us  [shards(): lax.all_gather(output_full, 'mp', axis=0, tiled=True)]
    all_gather x0 -> x1, local copies, waits for them, and re-layouts: none -> 8.63 us  [shape_sources_all(): return jnp.concatenate(all_gather(mine_x, peer_axis), axis=2)]
  transfers between devices with their start and end apart: 7 -> 7, of which waited for: 7 -> 7; matrix products, arithmetic and copies ran while one was open for 25% -> 28% of each run, Pallas kernels for 0% -> 0%
where the time goes in v1:
time: 338 us; the launch traced here: 337 us
  waiting for transfers between devices  208 us (62%)
  matrix products  57.4 us (17%)
  local copies, waits for them, and re-layouts  33.4 us (10%)
  other arithmetic  18.2 us (5%)
  between operations  13.7 us (4%)
  starting transfers between devices  5.93 us (2%)
    all_gather x1, waiting for transfers between devices, shards(): lax.all_gather(text_bank, ('dp', 'mp'), axis=0, tiled=True)  62.9 us
    all_gather x1, waiting for transfers between devices, gather_turned(): result, at, outs = (lax.all_gather(both, axis, axis=0, tiled=True), 0, [])  50.7 us
    all_gather x1, waiting for transfers between devices, shards(): lax.all_gather(up_full, 'mp', axis=1, tiled=True)  39.5 us
    all_gather x1, waiting for transfers between devices, shards(): lax.all_gather(down_full, 'mp', axis=0, tiled=True)  30.3 us
    all_gather x1, waiting for transfers between devices, shape_sources_all(): return jnp.concatenate(all_gather(mine_x, peer_axis), axis=2)  22.2 us
    dot_general x1, matrix products, shards(): upper = jnp.dot(normed_second, up_all, preferred_element_type=jnp.float32)  21.2 us
    dot_general x2, matrix products, grouped_local(): jnp.einsum('rgk,gkn->rgn', left_groups, right_groups, preferred_element_t...  15.4 us
    dot_general x1, matrix products, shards(): lax.dot_general(image_units, lax.all_gather(text_bank, ('dp', 'mp'), axis...  9.03 us
  transfers between devices with their start and end apart: 7, of which 7 were waited for; matrix products, arithmetic and copies ran while one was open for 28% of the time, Pallas kernels for 0%

profile of v1, /device:TPU:1, one launch (start us, length us, event | category | flops | bytes accessed | tf_op | source)
XLA Modules:
  0.0 336.8 jit_solution(6643877292453016603)
XLA Ops:
  7.5 1.6 pad_maximum_fusion
  9.1 50.7 %all-gather.7.cloned.1.call-done = bf16[1024,1536]{1,0:T(8,128)(2,1)} async-done(((bf16[64,1536]{1,0:T(8,128)(2,1)}), bf16[1024,1536]{1,0:T(8,128)(2,1)}) %all-gather.7.cloned.1.call-update) | async-done | bytes 3145744 | tf_op jit(solution)/shard_map/all_gather | solution.py:15
  59.8 1.2 slice.30
  61.3 1.2 copy.84
  62.6 1.0 slice.29
  64.5 2.7 fusion.42
  67.2 1.3 copy.106
  69.7 5.7 %all-to-all-start = ((f32[8,1,2]{2,1,0:T(1,128)}), f32[8,1,2]{2,1,0:T(1,128)S(1)}, u32[]{:S(2)}, u32[]{:S(2)}) async-start(f32[8,1,2]{2,1,0:T(1,128)} %broadcast_in_dim.5), calls=%async_computation | async-start | bytes 8192 | tf_op jit(solution)/shard_map/all_to_all | solution.py:31
  75.5 1.4 copy.94
  78.2 2.0 all-to-all-done
  81.4 22.2 %all-gather.11.cloned.1.call-done = bf16[8,1024,3,128]{3,1,2,0:T(8,128)(2,1)} async-done(((bf16[1,1024,3,128]{3,1,2,0:T(8,128)(2,1)}), bf16[8,1024,3,128]{3,1,2,0:T(8,128)(2,1)}) %all-gather.11.cloned.1.call-update) | async-done | bytes 6291472 | tf_op jit(solution)/shard_map/all_gather | solution.py:9
  103.6 8.6 %copy.85 = bf16[8,1024,3,128]{1,3,0,2:T(8,128)(2,1)} copy(bf16[8,1024,3,128]{3,1,2,0:T(8,128)(2,1)} %all-gather.11.cloned.1.call-done) | data formatting | bytes 12582912 | tf_op jit(solution)/shard_map/all_gather | solution.py:9
  112.2 8.2 %fusion.23 = f32[6,64,3,16,64]{1,4,3,2,0:T(8,128)S(1)} fusion(bf16[3,16,64,1024,1]{3,2,1,0,4:T(8,128)(2,1)} %bitcast.75, bf16[6,64,1024]{2,1,0:T(8,128)(2,1)S(1)} %copy-done.1, f32[1024]{0:T(1024)S(1)} %copy-done.5, f32[6,64]{1,0:T(8,128)S(1)} %add_rsqrt_fusion.3, f32[6,64]{1,0:T(8,128)S(1)} %broadcast_multiply_fusion.1), kind=kOutput, calls=%fused_computation.50 | convolution fusion | flops 2417885184 | bytes 11803648 | tf_op jit(solution)/shard_map/dot_general | solution.py:54
  120.4 1.2 multiply_reduce_fusion.1
  121.7 1.2 fusion.12
  122.8 2.0 fusion.19
  124.8 3.2 copy.89
  128.0 2.6 reshape_reshape.7
  130.8 3.5 %convert_bitcast_fusion.1 = bf16[384,8,1024]{0,2,1:T(8,128)(2,1)S(1)} fusion(bf16[8,128,1024]{2,1,0:T(8,128)(2,1)} %bitcast.79, bf16[384,8,128]{2,1,0:T(8,128)(2,1)S(1)} %reshape_reshape.7), kind=kOutput, calls=%fused_computation.20 | convolution fusion | flops 808452096 | bytes 9175040 | tf_op jit(solution)/shard_map/rgk,gkn->rgn/dot_general | solution.py:75
  134.3 2.0 convert_reduce_fusion.1
  136.3 3.0 copy.92
  139.3 1.6 fusion.33
  141.0 1.9 multiply_reduce_fusion.2
  143.0 39.5 %all-gather.15.cloned.1.call-done = bf16[1024,4096]{1,0:T(8,128)(2,1)} async-done(((bf16[1024,512]{1,0:T(8,128)(2,1)}), bf16[1024,4096]{1,0:T(8,128)(2,1)}) %all-gather.15.cloned.1.call-update) | async-done | bytes 8388624 | tf_op jit(solution)/shard_map/all_gather | solution.py:107
  182.5 21.2 %fusion.2 = bf16[384,4096]{1,0:T(8,128)(2,1)} fusion(bf16[1024,4096]{1,0:T(8,128)(2,1)} %all-gather.15.cloned.1.call-done, f32[384,1024]{0,1:T(8,128)} %copy.94, f32[384,1024]{0,1:T(8,128)} %convert_reduce_fusion.1, f32[1024]{0:T(1024)S(1)} %copy-done.6, f32[384]{0:T(512)S(1)} %rsqrt.55, f32[384]{0:T(512)S(1)} %div.39), kind=kOutput, calls=%fused_computation.5 | convolution fusion | flops 3325427712 | bytes 14687232 | tf_op jit(solution)/shard_map/dot_general | solution.py:116
  203.7 30.3 %all-gather.13.cloned.1.call-done = bf16[4096,1024]{1,0:T(8,128)(2,1)} async-done(((bf16[512,1024]{1,0:T(8,128)(2,1)}), bf16[4096,1024]{1,0:T(8,128)(2,1)}) %all-gather.13.cloned.1.call-update) | async-done | bytes 8388624 | tf_op jit(solution)/shard_map/all_gather | solution.py:108
  234.0 11.9 %convert_bitcast_fusion = bf16[384,8,1024]{0,2,1:T(8,128)(2,1)} fusion(bf16[8,512,1024]{2,1,0:T(8,128)(2,1)} %bitcast.83, bf16[48,8,8,512]{3,2,1,0:T(8,128)(2,1)} %bitcast.84), kind=kOutput, calls=%fused_computation.6 | convolution fusion | flops 3224371200 | bytes 17825792 | tf_op jit(solution)/shard_map/rgk,gkn->rgn/dot_general | solution.py:75
  245.9 5.1 %convert_reduce_fusion = f32[384,1024]{0,1:T(8,128)} fusion(bf16[384,8,1024]{0,2,1:T(8,128)(2,1)} %convert_bitcast_fusion), kind=kLoop, calls=%fused_computation | loop fusion | flops 5898240 | bytes 7864320 | tf_op jit(solution)/shard_map/reduce_sum | solution.py:79
  250.9 3.0 copy.97
  253.9 2.3 add_reduce_fusion
  257.1 62.9 %all-gather.17.cloned.1.call-done = bf16[12288,768]{1,0:T(8,128)(2,1)} async-done(((bf16[96,768]{1,0:T(8,128)(2,1)}), bf16[12288,768]{1,0:T(8,128)(2,1)}) %all-gather.17.cloned.1.call-update) | async-done | bytes 18874384 | tf_op jit(solution)/shard_map/all_gather | solution.py:131
  320.0 9.0 %fusion.43 = (f32[6]{0:T(128)S(1)}, f32[6,12288]{1,0:T(8,128)S(1)}) fusion(bf16[12288,768]{1,0:T(8,128)(2,1)} %all-gather.17.cloned.1.call-done, f32[6,768]{1,0:T(8,128)S(1)} %get-tuple-element.14, f32[6]{0:T(128)S(1)} %add_rsqrt_fusion.4), kind=kOutput, calls=%fused_computation.90 | convolution fusion | flops 113329144 | bytes 19187760 | tf_op jit(solution)/shard_map/dot_general | solution.py:129
  (53 shorter events, 8.1 us)
Async XLA Ops:
  6.5 250.1 %copy-start = (bf16[1024,768]{1,0:T(8,128)(2,1)S(1)}, bf16[1024,768]{1,0:T(8,128)(2,1)}, u32[]{:S(2)}) copy-start(bf16[1024,768]{1,0:T(8,128)(2,1)} %param.22) | copy-start | bytes 4718596
  6.5 53.2 %all-gather.7.cloned.1.call-start = ((), (), s32[]{:S(2)}) async-start(), calls=%async_computation.1 | async-start | bytes 3342336 | tf_op jit(solution)/shard_map/all_gather | solution.py:15
  9.1 94.5 %all-gather.11.cloned.1.call-start = ((), (), s32[]{:S(2)}) async-start(), calls=%async_computation.3 | async-start | bytes 7077888 | tf_op jit(solution)/shard_map/all_gather | solution.py:9
  61.3 7.9 %copy-start.3 = (f32[2]{0:T(128)S(1)}, f32[2]{0:T(128)}, u32[]{:S(2)}) copy-start(f32[2]{0:T(128)} %param.16) | copy-start | bytes 28
  61.3 14.2 %copy-start.1 = (bf16[6,64,1024]{2,1,0:T(8,128)(2,1)S(1)}, bf16[6,64,1024]{2,1,0:T(8,128)(2,1)}, u32[]{:S(2)}) copy-start(bf16[6,64,1024]{2,1,0:T(8,128)(2,1)} %param.13) | copy-start | bytes 2359300
  62.5 68.3 %all-gather.9.cloned.1.call-start = ((), (), s32[]{:S(2)}) async-start(), calls=%async_computation.2 | async-start | bytes 2359296 | tf_op jit(solution)/shard_map/all_gather | solution.py:106
  64.4 118.1 %all-gather.15.cloned.1.call-start = ((), (), s32[]{:S(2)}) async-start(), calls=%async_computation.5 | async-start | bytes 9437184 | tf_op jit(solution)/shard_map/all_gather | solution.py:107
  67.2 166.8 %all-gather.13.cloned.1.call-start = ((), (), s32[]{:S(2)}) async-start(), calls=%async_computation.4 | async-start | bytes 9437184 | tf_op jit(solution)/shard_map/all_gather | solution.py:108
  68.6 251.4 %all-gather.17.cloned.1.call-start = ((), (), s32[]{:S(2)}) async-start(), calls=%async_computation.6 | async-start | bytes 19021824 | tf_op jit(solution)/shard_map/all_gather | solution.py:131
  69.7 10.4 %all-to-all-start = ((f32[8,1,2]{2,1,0:T(1,128)}), f32[8,1,2]{2,1,0:T(1,128)S(1)}, u32[]{:S(2)}, u32[]{:S(2)}) async-start(f32[8,1,2]{2,1,0:T(1,128)} %broadcast_in_dim.5), calls=%async_computation | async-start | bytes 8192 | tf_op jit(solution)/shard_map/all_to_all | solution.py:31
  81.4 30.8 %copy-start.5 = (f32[1024]{0:T(1024)S(1)}, f32[1024]{0:T(1024)}, u32[]{:S(2)}) copy-start(f32[1024]{0:T(1024)} %param.14) | copy-start | bytes 12292
  134.3 48.2 %copy-start.6 = (f32[1024]{0:T(1024)S(1)}, f32[1024]{0:T(1024)}, u32[]{:S(2)}) copy-start(f32[1024]{0:T(1024)} %param.18) | copy-start | bytes 12292
  245.9 10.8 %copy-start.2 = (f32[1024]{0:T(1024)S(1)}, f32[1024]{0:T(1024)}, u32[]{:S(2)}) copy-start(f32[1024]{0:T(1024)} %param.21) | copy-start | bytes 12292
  320.0 9.4 %copy-start.4 = (f32[6]{0:T(128)S(1)}, f32[6]{0:T(128)}, u32[]{:S(2)}) copy-start(f32[6]{0:T(128)} %param.25) | copy-start | bytes 76
Sparse Core Ops, SparseCore 0:
  9.5 50.2 all-gather.6
  62.6 40.9 all-gather.10
  105.3 25.4 all-gather.8
  132.3 50.1 all-gather.14
  184.0 49.8 all-gather.12
  236.9 83.1 all-gather.16
